TPU v7x, 32 devices: a whole 2x2x4 slice. The times are simulated.
32 devices in a mesh: dp: 4 (over z), hid: 2 (over x), dm: 4 (over y, core).
Axes of the slice: x: 2, y: 2, z: 4, core: 2. Of those that a mesh axis runs over, the one named last changes fastest.
Arguments:
- tokens: bfloat16 [32768, 1024], P(('dp', 'hid', 'dm')), may hold values from -6 to 6
- first_values: bfloat16 [32768, 1024], P(('dp', 'hid', 'dm')), may hold values from -6 to 6
- doc_lengths: int32 [32, 8], P(('dp', 'hid', 'dm')), may hold values from 1 to 512, 1024 in all within a row
- cotangent: bfloat16 [32768, 1024], P(('dp', 'hid', 'dm')), may hold values from -6 to 6
- attn_gain: bfloat16 [1024], P(('dp', 'hid', 'dm')), may hold values from 0.25 to 1.75
- w_query: bfloat16 [1024, 1024], P(('dp', 'hid', 'dm')), may hold values from -0.1875 to 0.1875
- w_key: bfloat16 [1024, 1024], P(('dp', 'hid', 'dm')), may hold values from -0.1875 to 0.1875
- w_value: bfloat16 [1024, 1024], P(('dp', 'hid', 'dm')), may hold values from -0.1875 to 0.1875
- w_out: bfloat16 [1024, 1024], P(('dp', 'hid', 'dm')), may hold values from -1 to 1
- mlp_gain: bfloat16 [1024], P(('dp', 'hid', 'dm')), may hold values from 0.25 to 1.75
- w_gate: bfloat16 [1024, 2816], P(None, ('hid', 'dm')), may hold values from -0.1875 to 0.1875
- w_up: bfloat16 [1024, 2816], P(None, ('hid', 'dm')), may hold values from -0.1875 to 0.1875
- w_down: bfloat16 [2816, 1024], P(('hid', 'dm')), may hold values from -0.109375 to 0.109375
Outputs:
- output: bfloat16 [32768, 1024], P(('dp', 'hid', 'dm'))
- tokens_grad: bfloat16 [32768, 1024], P(('dp', 'hid', 'dm'))
- first_values_grad: bfloat16 [32768, 1024], P(('dp', 'hid', 'dm'))
- w_query_grad: float32 [1024, 1024], P(('dp', 'hid', 'dm'))
- w_key_grad: float32 [1024, 1024], P(('dp', 'hid', 'dm'))
- w_value_grad: float32 [1024, 1024], P(('dp', 'hid', 'dm'))
- w_out_grad: float32 [1024, 1024], P(('dp', 'hid', 'dm'))
- attn_gain_grad: float32 [1024], P(('dp', 'hid', 'dm'))
- mlp_gain_grad: float32 [1024], P(('dp', 'hid', 'dm'))
- w_gate_grad: float32 [1024, 2816], P(None, ('hid', 'dm'))
- w_up_grad: float32 [1024, 2816], P(None, ('hid', 'dm'))
- w_down_grad: float32 [2816, 1024], P(('hid', 'dm'))
Inputs may be any that keep to these rules, and one draw needn't show every extreme that they name: `doc_lengths`: each packed row's 8 document lengths sum to 1024, and every row holds one document of the maximum length.
All inputs are finite; a program needn't handle non-finite values.
Results may differ from a plain program's by a relative error of at most 0.017.
Values may be sent and summed in bfloat16 or wider, within the bound.
A program may use at most 192 MiB of HBM per device.

v0:
```python
import jax
import jax.numpy as jnp
from jax import lax
from jax.sharding import PartitionSpec as P

HD = 64
epsilon = 1e-06


def rms_scale(values, gain_vec):
    return (
        values * lax.rsqrt(jnp.mean(values * values, axis=-1, keepdims=True) + epsilon) * gain_vec
    )


def rope_tables(length, head_dim):
    half_dim = head_dim // 2
    places = jnp.arange(length).astype(jnp.float32)
    frequency = 10000.0 ** (-2.0 * jnp.arange(half_dim).astype(jnp.float32) / head_dim)
    angles = places[:, None] * frequency[None, :]
    return (jnp.cos(angles), jnp.sin(angles))


def rotate(values, cosine, sine_part):
    half_dim = values.shape[-1] // 2
    first_half = values[..., :half_dim]
    second_half = values[..., half_dim:]
    return jnp.concatenate(
        [
            first_half * cosine - second_half * sine_part,
            second_half * cosine + first_half * sine_part,
        ],
        axis=-1,
    )


def plain_dot(left_mat, right_mat):
    return jnp.dot(left_mat, right_mat, preferred_element_type=jnp.float32)


def contract_rows(left_mat, right_mat):
    return lax.dot_general(
        left_mat, right_mat, (((0,), (0,)), ((), ())), preferred_element_type=jnp.float32
    )


def contract_cols(left_mat, right_mat):
    return lax.dot_general(
        left_mat, right_mat, (((1,), (1,)), ((), ())), preferred_element_type=jnp.float32
    )


def swiglu(gate_in, up_in):
    return jax.nn.silu(gate_in) * up_in


def allowed_pairs(segment_row):
    places = jnp.arange(segment_row.shape[0])
    return (segment_row[:, None] == segment_row[None, :]) & (places[:, None] >= places[None, :])


def head_forward(head_items):
    query_head, key_head, value_head, segment_row = head_items
    score_scale = query_head.shape[-1] ** (-0.5)
    scores = jnp.where(
        allowed_pairs(segment_row), contract_cols(query_head, key_head) * score_scale, -1e30
    )
    row_max = jnp.max(scores, axis=-1, keepdims=True)
    weights_exp = jnp.exp(scores - row_max)
    row_total = jnp.sum(weights_exp, axis=-1, keepdims=True)
    weights_soft = weights_exp / row_total
    attended = plain_dot(weights_soft.astype(jnp.bfloat16), value_head)
    return (attended, row_max[:, 0] + jnp.log(row_total[:, 0]))


def head_backward(head_items):
    query_head, key_head, value_head, segment_row, grad_head, log_total = head_items
    score_scale = query_head.shape[-1] ** (-0.5)
    allowed = allowed_pairs(segment_row)
    scores = jnp.where(allowed, contract_cols(query_head, key_head) * score_scale, -1e30)
    weights_soft = jnp.where(allowed, jnp.exp(scores - log_total[:, None]), 0.0)
    grad_soft = contract_cols(grad_head, value_head)
    delta_row = jnp.sum(grad_soft * weights_soft, axis=-1, keepdims=True)
    grad_scores = (weights_soft * (grad_soft - delta_row)).astype(jnp.bfloat16)
    grad_query = plain_dot(grad_scores, key_head) * score_scale
    grad_key = contract_rows(grad_scores, query_head) * score_scale
    grad_mixed = contract_rows(weights_soft.astype(jnp.bfloat16), grad_head)
    return (grad_query, grad_key, grad_mixed)


def on_device(
    tokens,
    first_values,
    doc_lengths,
    cotangent,
    attn_gain,
    w_query,
    w_key,
    w_value,
    w_out,
    mlp_gain,
    w_gate,
    w_up,
    w_down,
):
    row_count = doc_lengths.shape[0]
    tok_count, model_width = tokens.shape
    length = tok_count // row_count
    head_count = model_width // HD
    full_query, full_key, full_value, full_out, gain_first, gain_second = (
        lax.all_gather(w_query, ("dp", "hid", "dm"), axis=0, tiled=True),
        lax.all_gather(w_key, ("dp", "hid", "dm"), axis=0, tiled=True),
        lax.all_gather(w_value, ("dp", "hid", "dm"), axis=0, tiled=True),
        lax.all_gather(w_out, ("dp", "hid", "dm"), axis=0, tiled=True),
        lax.all_gather(attn_gain, ("dp", "hid", "dm"), axis=0, tiled=True),
        lax.all_gather(mlp_gain, ("dp", "hid", "dm"), axis=0, tiled=True),
    )
    gain_one = gain_first.astype(jnp.float32)
    gain_two = gain_second.astype(jnp.float32)
    doc_ends = jnp.cumsum(doc_lengths, axis=1)
    places = jnp.arange(length)
    segments = jnp.sum((places[None, :, None] >= doc_ends[:, None, :]).astype(jnp.int32), axis=2)
    head_segments = jnp.repeat(segments, head_count, axis=0)
    cosine, sine_part = rope_tables(length, HD)
    cosine = cosine[:, None, :]
    sine_part = sine_part[:, None, :]

    def to_heads(flat_rows):
        return flat_rows.reshape(row_count, length, head_count, HD)

    def head_major(split_rows):
        return split_rows.transpose(0, 2, 1, 3).reshape(row_count * head_count, length, HD)

    def unheads(stacked):
        return stacked.reshape(row_count, head_count, length, HD).transpose(0, 2, 1, 3)

    inputs = tokens.astype(jnp.float32)
    normed = rms_scale(inputs, gain_one).astype(jnp.bfloat16)
    query_rot = head_major(
        rotate(to_heads(plain_dot(normed, full_query)), cosine, sine_part).astype(jnp.bfloat16)
    )
    key_rot = head_major(
        rotate(to_heads(plain_dot(normed, full_key)), cosine, sine_part).astype(jnp.bfloat16)
    )
    mixed_values = head_major(
        to_heads(
            (0.5 * plain_dot(normed, full_value) + 0.5 * first_values.astype(jnp.float32)).astype(
                jnp.bfloat16
            )
        )
    )
    attended, log_totals = lax.map(head_forward, (query_rot, key_rot, mixed_values, head_segments))
    attn_rows = unheads(attended).reshape(tok_count, model_width).astype(jnp.bfloat16)
    middle = inputs + plain_dot(attn_rows, full_out)
    normed_two = rms_scale(middle, gain_two).astype(jnp.bfloat16)
    gate_full, up_full, down_full = (
        lax.all_gather(w_gate, ("hid", "dm"), axis=1, tiled=True),
        lax.all_gather(w_up, ("hid", "dm"), axis=1, tiled=True),
        lax.all_gather(w_down, ("hid", "dm"), axis=0, tiled=True),
    )
    hidden_f, silu_back = jax.vjp(
        swiglu, plain_dot(normed_two, gate_full), plain_dot(normed_two, up_full)
    )
    hidden = hidden_f.astype(jnp.bfloat16)
    mlp_result = plain_dot(hidden, down_full)
    grad_gate_f, grad_up_f = silu_back(contract_cols(cotangent, down_full))
    grad_gate_act = grad_gate_f.astype(jnp.bfloat16)
    grad_up_act = grad_up_f.astype(jnp.bfloat16)
    grad_normed_two = contract_cols(grad_gate_act, gate_full) + contract_cols(grad_up_act, up_full)
    local_gate = contract_rows(normed_two, grad_gate_act)
    local_up = contract_rows(normed_two, grad_up_act)
    local_down = contract_rows(hidden, cotangent)
    output = (middle + mlp_result).astype(jnp.bfloat16)
    norm_two_value, norm_two_back = jax.vjp(rms_scale, middle, gain_two)
    grad_mid_norm, grad_gain_two = norm_two_back(grad_normed_two)
    grad_middle = cotangent.astype(jnp.float32) + grad_mid_norm
    grad_branch = grad_middle.astype(jnp.bfloat16)
    back_query, back_key, back_value, back_out, back_first = (
        lax.all_gather(w_query, ("dp", "hid", "dm"), axis=0, tiled=True),
        lax.all_gather(w_key, ("dp", "hid", "dm"), axis=0, tiled=True),
        lax.all_gather(w_value, ("dp", "hid", "dm"), axis=0, tiled=True),
        lax.all_gather(w_out, ("dp", "hid", "dm"), axis=0, tiled=True),
        lax.all_gather(attn_gain, ("dp", "hid", "dm"), axis=0, tiled=True),
    )
    back_gain = back_first.astype(jnp.float32)
    out_grad = contract_rows(attn_rows, grad_branch)
    grad_attended = head_major(to_heads(contract_cols(grad_branch, back_out).astype(jnp.bfloat16)))
    grad_query_rot, grad_key_rot, grad_mixed = lax.map(
        head_backward, (query_rot, key_rot, mixed_values, head_segments, grad_attended, log_totals)
    )
    grad_query_rows = (
        rotate(unheads(grad_query_rot), cosine, -sine_part)
        .reshape(tok_count, model_width)
        .astype(jnp.bfloat16)
    )
    grad_key_rows = (
        rotate(unheads(grad_key_rot), cosine, -sine_part)
        .reshape(tok_count, model_width)
        .astype(jnp.bfloat16)
    )
    values_grad = (0.5 * unheads(grad_mixed).reshape(tok_count, model_width)).astype(jnp.bfloat16)
    query_grad = contract_rows(normed, grad_query_rows)
    key_grad = contract_rows(normed, grad_key_rows)
    value_w_grad = contract_rows(normed, values_grad)
    grad_normed = (
        contract_cols(grad_query_rows, back_query)
        + contract_cols(grad_key_rows, back_key)
        + contract_cols(values_grad, back_value)
    )
    norm_one_value, norm_one_back = jax.vjp(rms_scale, inputs, back_gain)
    grad_in_norm, grad_gain_one = norm_one_back(grad_normed)
    tokens_grad = (grad_middle + grad_in_norm).astype(jnp.bfloat16)
    part_gate, part_up, part_down = (
        lax.psum_scatter(
            local_gate.astype(jnp.bfloat16), ("hid", "dm"), scatter_dimension=1, tiled=True
        ).astype(jnp.float32),
        lax.psum_scatter(
            local_up.astype(jnp.bfloat16), ("hid", "dm"), scatter_dimension=1, tiled=True
        ).astype(jnp.float32),
        lax.psum_scatter(
            local_down.astype(jnp.bfloat16), ("hid", "dm"), scatter_dimension=0, tiled=True
        ).astype(jnp.float32),
    )
    gate_grad, up_grad, down_grad = (
        lax.psum(part_gate.astype(jnp.bfloat16), "dp").astype(jnp.float32),
        lax.psum(part_up.astype(jnp.bfloat16), "dp").astype(jnp.float32),
        lax.psum(part_down.astype(jnp.bfloat16), "dp").astype(jnp.float32),
    )
    query_sum, key_sum, value_sum, out_sum, gain_one_sum, gain_two_sum = (
        lax.psum_scatter(query_grad, ("dp", "hid", "dm"), scatter_dimension=0, tiled=True),
        lax.psum_scatter(key_grad, ("dp", "hid", "dm"), scatter_dimension=0, tiled=True),
        lax.psum_scatter(value_w_grad, ("dp", "hid", "dm"), scatter_dimension=0, tiled=True),
        lax.psum_scatter(out_grad, ("dp", "hid", "dm"), scatter_dimension=0, tiled=True),
        lax.psum_scatter(grad_gain_one, ("dp", "hid", "dm"), scatter_dimension=0, tiled=True),
        lax.psum_scatter(grad_gain_two, ("dp", "hid", "dm"), scatter_dimension=0, tiled=True),
    )
    return (
        output,
        tokens_grad,
        values_grad,
        query_sum,
        key_sum,
        value_sum,
        out_sum,
        gain_one_sum,
        gain_two_sum,
        gate_grad,
        up_grad,
        down_grad,
    )


def solution(mesh):
    return jax.shard_map(
        on_device,
        mesh=mesh,
        in_specs=(
            P(("dp", "hid", "dm"), None),
            P(("dp", "hid", "dm"), None),
            P(("dp", "hid", "dm"), None),
            P(("dp", "hid", "dm"), None),
            P(("dp", "hid", "dm")),
            P(("dp", "hid", "dm"), None),
            P(("dp", "hid", "dm"), None),
            P(("dp", "hid", "dm"), None),
            P(("dp", "hid", "dm"), None),
            P(("dp", "hid", "dm")),
            P(None, ("hid", "dm")),
            P(None, ("hid", "dm")),
            P(("hid", "dm"), None),
        ),
        out_specs=(
            P(("dp", "hid", "dm"), None),
            P(("dp", "hid", "dm"), None),
            P(("dp", "hid", "dm"), None),
            P(("dp", "hid", "dm"), None),
            P(("dp", "hid", "dm"), None),
            P(("dp", "hid", "dm"), None),
            P(("dp", "hid", "dm"), None),
            P(("dp", "hid", "dm")),
            P(("dp", "hid", "dm")),
            P(None, ("hid", "dm")),
            P(None, ("hid", "dm")),
            P(("hid", "dm"), None),
        ),
        check_vma=False,
    )
```

profile of v0, /device:TPU:0, one launch (start us, length us, event | category | flops | bytes accessed | tf_op | source)
XLA Modules:
  0.0 1386.8 jit_solution(16985763490271452871)
XLA Ops:
  17.5 42.0 %all-reduce.5 = (bf16[1024]{0:T(1024)(128)(2,1)S(1)}, bf16[1024]{0:T(1024)(128)(2,1)S(1)}) all-reduce(bf16[1024]{0:T(1024)(128)(2,1)S(1)} %dynamic-update-slice, bf16[1024]{0:T(1024)(128)(2,1)S(1)} %dynamic-update-slice.1), channel_id=1, replica_groups=mesh['dp'=4,'hid'=2,'dm'=4] {'dp','hid','dm'}, use_global_device_ids=true, to_apply=%add | all-reduce | flops 2048 | bytes 8192
  59.5 4.0 copy.80
  65.0 5.0 all-gather.8.cloned.1.call-done
  70.0 6.1 fusion.74
  76.0 52.0 %all-gather.10.cloned.1.call-done = bf16[1024,1024]{1,0:T(8,128)(2,1)} async-done(((bf16[32,1024]{1,0:T(8,128)(2,1)}), bf16[1024,1024]{1,0:T(8,128)(2,1)}) %all-gather.10.cloned.1.call-update) | async-done | bytes 2097168 | tf_op jit(solution)/shard_map/all_gather | solution.py:112
  128.1 4.3 fusion.72
  136.4 4.8 copy.82
  141.2 4.7 copy.83
  145.9 40.2 %all-gather.12.cloned.1.call-done = bf16[1024,1024]{1,0:T(8,128)(2,1)} async-done(((bf16[32,1024]{1,0:T(8,128)(2,1)}), bf16[1024,1024]{1,0:T(8,128)(2,1)}) %all-gather.12.cloned.1.call-update) | async-done | bytes 2097168 | tf_op jit(solution)/shard_map/all_gather | solution.py:113
  186.1 6.2 multiply_convert_fusion.5
  192.3 5.2 copy.81
  197.5 136.9 %while.28 = (s32[]{:T(128)}, bf16[16,1024,64]{1,2,0:T(8,128)(2,1)}, f32[16,1024]{1,0:T(8,128)S(1)}, s32[16,1024]{1,0:T(8,128)S(1)}, bf16[16,1024,64]{2,1,0:T(8,1...) while((s32[]{:T(128)}, bf16[16,1024,64]{1,2,0:T(8,128)(2,1)}, ...), condition=%wide.region_6.7_spmd.clone, body=%wide.region_3.6_spmd.sunk.clone | while | flops 279968768 | bytes 30468208 | solution.py:152
  210.8 3.8 fusion.151
  219.4 3.8 fusion.151
  227.9 4.0 fusion.151
  236.7 3.8 fusion.151
  296.2 4.1 fusion.151
  313.6 3.8 fusion.151
  330.6 3.8 fusion.151
  334.5 4.8 multiply_reduce_fusion.3
  343.0 11.7 fusion.77
  354.7 12.2 fusion.78
  366.9 10.9 all-gather.20.cloned.1.call-done
  377.8 21.6 %multiply_convert_fusion.1 = (bf16[1024,2816]{1,0:T(8,128)(2,1)}, bf16[1024,2816]{1,0:T(8,128)(2,1)}, bf16[1024,2816]{1,0:T(8,128)(2,1)}) fusion(f32[1024,2816]{1,0:T(8,128)} %fusion.77, f32[1024,2816]{1,0:T(8,128)} %fusion.78, bf16[1024,1024]{1,0:T(8,128)(2,1)S(1)} %copy-done.10, bf16[2816,1024]{1,0:T(8,128)(2,1)} %all-gather.20.cloned.1.call-done), kind=kOutput, calls=%fused_computation.60 | convolution fusion | flops 5951717376 | bytes 48234496 | tf_op jit(solution)/shard_map/dot_general | solution.py:48
  399.4 11.0 convolution_convert_fusion.2
  410.5 11.3 convolution_convert_fusion.1
  421.8 11.3 convolution_convert_fusion
  436.8 11.4 fusion.79
  448.2 11.3 multiply_reduce_fusion.1
  469.6 62.5 %reduce-scatter.18.cloned.1.call-done = bf16[1024,352]{0,1:T(8,128)(2,1)} async-done(((bf16[1024,2816]{0,1:T(8,128)(2,1)}), bf16[1024,352]{0,1:T(8,128)(2,1)}) %reduce-scatter.18.cloned.1.call-update) | async-done | bytes 720912 | tf_op jit(solution)/shard_map/reduce_scatter | solution.py:217
  532.1 62.3 %reduce-scatter.20.cloned.1.call-done = bf16[352,1024]{1,0:T(8,128)(2,1)} async-done(((bf16[2816,1024]{1,0:T(8,128)(2,1)}), bf16[352,1024]{1,0:T(8,128)(2,1)}) %reduce-scatter.20.cloned.1.call-update) | async-done | bytes 720912 | tf_op jit(solution)/shard_map/reduce_scatter | solution.py:220
  594.5 205.6 %while.29 = (s32[]{:T(128)}, f32[16,1024,64]{1,2,0:T(8,128)}, f32[16,1024,64]{1,2,0:T(8,128)}, f32[16,1024,64]{1,2,0:T(8,128)}, s32[16,1024]{1,0:T(8,128)S(1)}, ...) while((s32[]{:T(128)}, f32[16,1024,64]{1,2,0:T(8,128)}, ...), condition=%wide.region_11.12_spmd.clone, body=%wide.region_9.11_spmd.sunk.clone | while | flops 684850176 | bytes 34120812 | solution.py:188
  800.1 5.8 subtract_convert_fusion
  808.3 4.4 fusion.67
  815.5 4.3 fusion.69
  819.9 7.2 fusion.59
  831.5 4.3 fusion.65
  835.9 4.0 copy.96
  839.8 4.7 fusion.81
  846.9 5.1 fusion.53
  852.1 40.4 %all-reduce.4 = (f32[1024]{0:T(1024)S(1)}, f32[1024]{0:T(1024)S(1)}) all-reduce(f32[1024]{0:T(1024)S(1)} %get-tuple-element.227, f32[1024]{0:T(1024)S(1)} %get-tuple-element.225), channel_id=6, replica_groups=mesh['dp'=4,'hid'=2,'dm'=4] {'dp','hid','dm'}, use_global_device_ids=true, to_apply=%region_18.19.clone | all-reduce | flops 2048 | bytes 16384
  893.6 5.9 fusion.56
  899.5 3.9 copy.95
  903.5 10.6 add_convert_fusion
  922.7 32.8 %reduce-scatter.10.cloned.1.call-done = f32[32,1024]{1,0:T(8,128)} async-done(((f32[1024,1024]{1,0:T(8,128)}), f32[32,1024]{1,0:T(8,128)}) %reduce-scatter.10.cloned.1.call-update) | async-done | bytes 131088 | tf_op jit(solution)/shard_map/reduce_scatter | solution.py:231
  955.6 141.6 %reduce-scatter.8.cloned.1.call-done = f32[32,1024]{1,0:T(8,128)} async-done(((f32[1024,1024]{1,0:T(8,128)}), f32[32,1024]{1,0:T(8,128)}) %reduce-scatter.8.cloned.1.call-update) | async-done | bytes 131088 | tf_op jit(solution)/shard_map/reduce_scatter | solution.py:230
  1097.2 141.5 %reduce-scatter.14.cloned.1.call-done = f32[32,1024]{1,0:T(8,128)} async-done(((f32[1024,1024]{1,0:T(8,128)}), f32[32,1024]{1,0:T(8,128)}) %reduce-scatter.14.cloned.1.call-update) | async-done | bytes 131088 | tf_op jit(solution)/shard_map/reduce_scatter | solution.py:233
  1238.6 141.2 %reduce-scatter.12.cloned.1.call-done = f32[32,1024]{1,0:T(8,128)} async-done(((f32[1024,1024]{1,0:T(8,128)}), f32[32,1024]{1,0:T(8,128)}) %reduce-scatter.12.cloned.1.call-update) | async-done | bytes 131088 | tf_op jit(solution)/shard_map/reduce_scatter | solution.py:232
  (382 shorter events, 369.0 us)
Async XLA Ops:
  7.2 62.8 %all-gather.8.cloned.1.call-start = ((), (), s32[]{:S(2)}) async-start(), calls=%async_computation.7 | async-start | bytes 2162688 | tf_op jit(solution)/shard_map/all_gather | solution.py:111
  7.9 120.1 %all-gather.10.cloned.1.call-start = ((), (), s32[]{:S(2)}) async-start(), calls=%async_computation.8 | async-start | bytes 2162688 | tf_op jit(solution)/shard_map/all_gather | solution.py:112
  8.7 177.4 %all-gather.12.cloned.1.call-start = ((), (), s32[]{:S(2)}) async-start(), calls=%async_computation.9 | async-start | bytes 2162688 | tf_op jit(solution)/shard_map/all_gather | solution.py:113
  9.4 325.1 %all-gather.14.cloned.1.call-start = ((), (), s32[]{:S(2)}) async-start(), calls=%async_computation.10 | async-start | bytes 2162688 | tf_op jit(solution)/shard_map/all_gather | solution.py:114
  10.0 331.7 %all-gather.16.cloned.1.call-start = ((), (), s32[]{:S(2)}) async-start(), calls=%async_computation.11 | async-start | bytes 6488064 | tf_op jit(solution)/shard_map/all_gather | solution.py:157
  10.6 344.1 %all-gather.18.cloned.1.call-start = ((), (), s32[]{:S(2)}) async-start(), calls=%async_computation.12 | async-start | bytes 6488064 | tf_op jit(solution)/shard_map/all_gather | solution.py:158
  11.1 366.7 %all-gather.20.cloned.1.call-start = ((), (), s32[]{:S(2)}) async-start(), calls=%async_computation.13 | async-start | bytes 6488064 | tf_op jit(solution)/shard_map/all_gather | solution.py:159
  11.9 457.7 %reduce-scatter.16.cloned.1.call-start = ((), (), s32[]{:S(2)}) async-start(), calls=%async_computation.18 | async-start | bytes 6488064 | tf_op jit(solution)/shard_map/reduce_scatter | solution.py:214
  12.0 5.0 copy-start.27
  12.0 5.3 copy-start.28
  16.4 318.1 %copy-start.1 = (bf16[1024,1024]{0,1:T(8,128)(2,1)}, bf16[1024,1024]{0,1:T(8,128)(2,1)S(1)}, u32[]{:S(2)}) copy-start(bf16[1024,1024]{0,1:T(8,128)(2,1)S(1)} %copy.79) | copy-start | bytes 6291460
  16.4 47.0 %copy-start.29 = (s32[1,8]{1,0:T(1,128)S(1)}, s32[1,8]{1,0:T(1,128)}, u32[]{:S(2)}) copy-start(s32[1,8]{1,0:T(1,128)} %param.19) | copy-start | bytes 100
  16.9 46.8 %copy-start.23 = (f32[1024]{0:T(1024)}, f32[1024]{0:T(1024)S(1)}, u32[]{:S(2)}) copy-start(f32[1024]{0:T(1024)S(1)} %fusion.57) | copy-start | bytes 12292
  16.9 169.1 %copy-start.21 = (f32[1024]{0:T(1024)}, f32[1024]{0:T(1024)S(1)}, u32[]{:S(2)}) copy-start(f32[1024]{0:T(1024)S(1)} %fusion.63) | copy-start | bytes 12292
  59.5 126.6 %copy-start.19 = (f32[1024]{0:T(1024)}, f32[1024]{0:T(1024)S(1)}, u32[]{:S(2)}) copy-start(f32[1024]{0:T(1024)S(1)} %convert_element_type.216) | copy-start | bytes 12292
  65.0 67.5 %copy-start.15 = (f32[1024,32]{0,1:T(8,128)}, f32[1024,32]{0,1:T(8,128)S(1)}, u32[]{:S(2)}) copy-start(f32[1024,32]{0,1:T(8,128)S(1)} %get-tuple-element.291) | copy-start | bytes 393220
  128.1 4.4 copy-start.9
  199.6 2.0 copy-start
  208.1 2.0 copy-start
  216.6 2.0 copy-start
  225.2 2.0 copy-start
  233.9 2.0 copy-start
  242.5 2.0 copy-start
  251.0 2.0 copy-start
  268.0 2.0 copy-start
  276.5 2.0 copy-start
  285.0 2.0 copy-start
  354.7 23.1 %copy-start.10 = (bf16[1024,1024]{1,0:T(8,128)(2,1)S(1)}, bf16[1024,1024]{1,0:T(8,128)(2,1)}, u32[]{:S(2)}) copy-start(bf16[1024,1024]{1,0:T(8,128)(2,1)} %param.20) | copy-start | bytes 6291460
  410.4 121.6 %reduce-scatter.18.cloned.1.call-start = ((), (), s32[]{:S(2)}) async-start(), calls=%async_computation.19 | async-start | bytes 6488064 | tf_op jit(solution)/shard_map/reduce_scatter | solution.py:217
  421.8 172.6 %reduce-scatter.20.cloned.1.call-start = ((), (), s32[]{:S(2)}) async-start(), calls=%async_computation.20 | async-start | bytes 6488064 | tf_op jit(solution)/shard_map/reduce_scatter | solution.py:220
  433.2 483.5 %all-reduce.9.cloned.1.call-start = ((), (), s32[]{:S(2)}) async-start(), calls=%async_computation.21 | async-start | bytes 4325376 | tf_op jit(solution)/shard_map/psum | solution.py:225
  436.8 11.4 copy-start.7
  461.2 2.3 copy-start.5
  594.4 361.2 %reduce-scatter.10.cloned.1.call-start = ((), (), s32[]{:S(2)}) async-start(), calls=%async_computation.15 | async-start | bytes 4325376 | tf_op jit(solution)/shard_map/reduce_scatter | solution.py:231
  594.4 205.7 %copy-start.16 = (f32[1024,32]{0,1:T(8,128)S(1)}, f32[1024,32]{0,1:T(8,128)}, u32[]{:S(2)}) copy-start(f32[1024,32]{0,1:T(8,128)} %copy-done.15) | copy-start | bytes 393220
  594.5 205.6 %copy-start.18 = (f32[1024,32]{0,1:T(8,128)S(1)}, f32[1024,32]{0,1:T(8,128)}, u32[]{:S(2)}) copy-start(f32[1024,32]{0,1:T(8,128)} %get-tuple-element.289) | copy-start | bytes 393220
  805.9 2.3 copy-start.2
  805.9 2.3 copy-start.20
  805.9 2.3 copy-start.22
  812.7 284.5 %reduce-scatter.8.cloned.1.call-start = ((), (), s32[]{:S(2)}) async-start(), calls=%async_computation.14 | async-start | bytes 4325376 | tf_op jit(solution)/shard_map/reduce_scatter | solution.py:230
  819.9 418.8 %reduce-scatter.14.cloned.1.call-start = ((), (), s32[]{:S(2)}) async-start(), calls=%async_computation.17 | async-start | bytes 4325376 | tf_op jit(solution)/shard_map/reduce_scatter | solution.py:233
  827.1 552.7 %reduce-scatter.12.cloned.1.call-start = ((), (), s32[]{:S(2)}) async-start(), calls=%async_computation.16 | async-start | bytes 4325376 | tf_op jit(solution)/shard_map/reduce_scatter | solution.py:232
  839.8 4.7 copy-start.13
  839.8 4.7 copy-start.25
  844.6 2.4 copy-start.4
  844.6 2.4 copy-start.8
  846.9 46.6 %copy-start.24 = (f32[1024]{0:T(1024)S(1)}, f32[1024]{0:T(1024)}, u32[]{:S(2)}) copy-start(f32[1024]{0:T(1024)} %copy-done.23) | copy-start | bytes 12292
  916.7 4.8 copy-start.17
  (12 other events, 20.7 us)
Sparse Core Ops, SparseCore 0:
  10.8 59.0 all-gather.7
  72.8 55.1 all-gather.9
  130.9 55.0 all-gather.11
  188.8 55.1 all-gather.13
  245.7 42.0 all-gather.15
  289.5 43.1 all-gather.17
  334.6 43.1 all-gather.19
  410.5 58.9 reduce-scatter.15
  473.0 58.9 reduce-scatter.17
  535.3 58.9 reduce-scatter.19
  597.0 88.2 all-reduce.8
  812.8 142.6 reduce-scatter.9
  958.4 138.6 reduce-scatter.7
  1099.9 138.7 reduce-scatter.13
  1241.3 138.4 reduce-scatter.11
where the time goes:
time: 1400 us; the launch traced here: 1390 us
  waiting for transfers between devices  697 us (50%)
  matrix products  448 us (32%)
  blocking collectives  82.4 us (6%)
  local copies, waits for them, and re-layouts  82.3 us (6%)
  other arithmetic  59.5 us (4%)
  between operations  14.8 us (1%)
    dot_general x55, matrix products, contract_cols(): lax.dot_general(left_mat, right_mat, (((1,), (1,)), ((), ())), preferred_...  165 us
    dot_general x39, matrix products, plain_dot(): return jnp.dot(left_mat, right_mat, preferred_element_type=jnp.float32)  152 us
    reduce_scatter x1, waiting for transfers between devices, on_device(): lax.psum_scatter(query_grad, ('dp', 'hid', 'dm'), scatter_dimension=0, ti...  142 us
    reduce_scatter x1, waiting for transfers between devices, on_device(): lax.psum_scatter(out_grad, ('dp', 'hid', 'dm'), scatter_dimension=0, tile...  141 us
    reduce_scatter x1, waiting for transfers between devices, on_device(): lax.psum_scatter(value_w_grad, ('dp', 'hid', 'dm'), scatter_dimension=0,...  141 us
    dot_general x39, matrix products, contract_rows(): lax.dot_general(left_mat, right_mat, (((0,), (0,)), ((), ())), preferred_...  132 us
    unnamed x2, blocking collectives  82.4 us
    reduce_scatter x1, waiting for transfers between devices, on_device(): lax.psum_scatter(local_up.astype(jnp.bfloat16), ('hid', 'dm'), scatter_di...  62.5 us
  transfers between devices with their start and end apart: 15, of which 11 were waited for; matrix products, arithmetic and copies ran while one was open for 37% of the time, Pallas kernels for 0%

commit v1 on v0

--- a/solution.py
+++ b/solution.py
@@ -1,3 +1,4 @@
+import functools
 import jax
 import jax.numpy as jnp
 from jax import lax
@@ -5,6 +6,29 @@
 
 HD = 64
 epsilon = 1e-06
+
+
+def attach_the_rates(vals, along_axis, along_dim):
+    then, state_now, prior = (
+        lax.axis_size(along_axis),
+        lax.axis_index(along_axis),
+        vals.shape[along_dim],
+    )
+    state_next, new = (vals, 1)
+    while new < then:
+        state_next = jnp.concatenate(
+            [
+                state_next,
+                lax.ppermute(state_next, along_axis, [(d, (d - new) % then) for d in range(then)]),
+            ],
+            axis=along_dim,
+        )
+        new = 2 * new
+    y = jnp.roll(state_next, shift=state_now * prior, axis=along_dim)
+    return y
+
+
+show_point = functools.partial(attach_the_rates, along_axis=("dp", "hid", "dm"), along_dim=0)
 
 
 def rms_scale(values, gain_vec):
@@ -110,7 +134,7 @@
     full_query, full_key, full_value, full_out, gain_first, gain_second = (
         lax.all_gather(w_query, ("dp", "hid", "dm"), axis=0, tiled=True),
         lax.all_gather(w_key, ("dp", "hid", "dm"), axis=0, tiled=True),
-        lax.all_gather(w_value, ("dp", "hid", "dm"), axis=0, tiled=True),
+        show_point(w_value),
         lax.all_gather(w_out, ("dp", "hid", "dm"), axis=0, tiled=True),
         lax.all_gather(attn_gain, ("dp", "hid", "dm"), axis=0, tiled=True),
         lax.all_gather(mlp_gain, ("dp", "hid", "dm"), axis=0, tiled=True),

time: 1400 us -> 1320 us (0.943)
  waiting for transfers between devices: 697 us -> 554 us
  local copies, waits for them, and re-layouts: 82.3 us -> 127 us
    reduce_scatter x1, waiting for transfers between devices: 141 us -> 0.01 us  [on_device(): lax.psum_scatter(out_grad, ('dp', 'hid', 'dm'), scatter_dimension=0, tile...]
    reduce_scatter x1, waiting for transfers between devices: 2.9 us -> 62.5 us  [on_device(): lax.psum_scatter(local_gate.astype(jnp.bfloat16), ('hid', 'dm'), scatter_...]
    ppermute x0 -> x5, waiting for transfers between devices: none -> 58.5 us  [attach_the_rates(): lax.ppermute(state_next, along_axis, [(d, (d - new) % then) for d in rang...]
    all_gather x1, waiting for transfers between devices: 52 us -> 8.29 us  [on_device(): lax.all_gather(w_key, ('dp', 'hid', 'dm'), axis=0, tiled=True)]
    reduce_scatter x1, waiting for transfers between devices: 62.5 us -> 21.1 us  [on_device(): lax.psum_scatter(local_up.astype(jnp.bfloat16), ('hid', 'dm'), scatter_di...]
    all_gather x1, waiting for transfers between devices: 40.2 us -> 0.01 us  [on_device(): lax.all_gather(w_value, ('dp', 'hid', 'dm'), axis=0, tiled=True)]
    reduce_scatter x1, waiting for transfers between devices: 32.8 us -> 54.9 us  [on_device(): lax.psum_scatter(key_grad, ('dp', 'hid', 'dm'), scatter_dimension=0, tile...]
    dynamic_update_slice x16, local copies, waits for them, and re-layouts: 1.72 us -> 22.4 us  [on_device(): lax.map(head_forward, (query_rot, key_rot, mixed_values, head_segments))]
  transfers between devices with their start and end apart: 15 -> 20, of which waited for: 11 -> 11; matrix products, arithmetic and copies ran while one was open for 37% -> 44% of each run, Pallas kernels for 0% -> 0%
where the time goes in v1:
time: 1320 us; the launch traced here: 1310 us
  waiting for transfers between devices  554 us (42%)
  matrix products  455 us (34%)
  local copies, waits for them, and re-layouts  127 us (10%)
  blocking collectives  80.4 us (6%)
  other arithmetic  62.9 us (5%)
  between operations  15 us (1%)
  starting transfers between devices  13.3 us (1%)
    dot_general x55, matrix products, contract_cols(): lax.dot_general(left_mat, right_mat, (((1,), (1,)), ((), ())), preferred_...  174 us
    dot_general x39, matrix products, plain_dot(): return jnp.dot(left_mat, right_mat, preferred_element_type=jnp.float32)  149 us
    reduce_scatter x1, waiting for transfers between devices, on_device(): lax.psum_scatter(query_grad, ('dp', 'hid', 'dm'), scatter_dimension=0, ti...  141 us
    reduce_scatter x1, waiting for transfers between devices, on_device(): lax.psum_scatter(value_w_grad, ('dp', 'hid', 'dm'), scatter_dimension=0,...  141 us
    dot_general x39, matrix products, contract_rows(): lax.dot_general(left_mat, right_mat, (((0,), (0,)), ((), ())), preferred_...  132 us
    unnamed x2, blocking collectives  80.4 us
    reduce_scatter x1, waiting for transfers between devices, on_device(): lax.psum_scatter(local_down.astype(jnp.bfloat16), ('hid', 'dm'), scatter_...  62.5 us
    reduce_scatter x1, waiting for transfers between devices, on_device(): lax.psum_scatter(local_gate.astype(jnp.bfloat16), ('hid', 'dm'), scatter_...  62.5 us
  transfers between devices with their start and end apart: 20, of which 11 were waited for; matrix products, arithmetic and copies ran while one was open for 44% of the time, Pallas kernels for 0%

profile of v1, /device:TPU:0, one launch (start us, length us, event | category | flops | bytes accessed | tf_op | source)
XLA Modules:
  0.0 1308.9 jit_solution(17823221114631650567)
XLA Ops:
  10.6 6.5 collective-permute-start
  20.8 4.6 collective-permute-done.1
  26.7 7.5 collective-permute-done.2
  41.4 40.5 %all-reduce.5 = (bf16[1024]{0:T(1024)(128)(2,1)S(1)}, bf16[1024]{0:T(1024)(128)(2,1)S(1)}) all-reduce(bf16[1024]{0:T(1024)(128)(2,1)S(1)} %dynamic-update-slice, bf16[1024]{0:T(1024)(128)(2,1)S(1)} %dynamic-update-slice.1), channel_id=1, replica_groups=mesh['dp'=4,'hid'=2,'dm'=4] {'dp','hid','dm'}, use_global_device_ids=true, to_apply=%add | all-reduce | flops 2048 | bytes 8192
  81.9 3.9 copy.80
  93.3 44.2 %collective-permute-done.4 = bf16[512,1024]{1,0:T(8,128)(2,1)S(1)} collective-permute-done((bf16[512,1024]{1,0:T(8,128)(2,1)S(1)}, bf16[512,1024]{1,0:T(8,128)(2,1)S(1)}, u32[]{:S(2)}, u32[]{:S(2)}) %collective-permute-start.4) | collective-permute-done | bytes 1048608 | tf_op jit(solution)/shard_map/ppermute | solution.py:22
  137.8 4.2 multiply_convert_fusion.5
  142.0 4.9 copy.81
  146.9 6.0 fusion.79
  153.0 8.3 all-gather.10.cloned.1.call-done
  161.3 4.3 fusion.77
  169.6 4.8 copy.82
  174.3 4.8 copy.83
  179.1 157.1 %while.28 = (s32[]{:T(128)}, bf16[16,1024,64]{1,2,0:T(8,128)(2,1)}, f32[16,1024]{1,0:T(8,128)}, s32[16,1024]{1,0:T(8,128)S(1)}, bf16[16,1024,64]{2,1,0:T(8,128)(...) while((s32[]{:T(128)}, bf16[16,1024,64]{1,2,0:T(8,128)(2,1)}, ...), condition=%wide.region_6.7_spmd.clone, body=%wide.region_3.6_spmd.sunk.clone | while | flops 279968768 | bytes 30468208 | solution.py:176
  243.8 3.9 fusion.155
  253.7 3.8 fusion.155
  273.2 3.8 fusion.155
  302.6 3.8 fusion.155
  331.9 4.1 fusion.155
  336.2 4.8 multiply_reduce_fusion.3
  344.7 11.6 fusion.82
  356.3 12.0 fusion.83
  368.4 21.9 %multiply_convert_fusion.1 = (bf16[1024,2816]{1,0:T(8,128)(2,1)}, bf16[1024,2816]{1,0:T(8,128)(2,1)}, bf16[1024,2816]{1,0:T(8,128)(2,1)}) fusion(f32[1024,2816]{1,0:T(8,128)} %fusion.82, f32[1024,2816]{1,0:T(8,128)} %fusion.83, bf16[1024,1024]{1,0:T(8,128)(2,1)S(1)} %copy-done.9, bf16[2816,1024]{1,0:T(8,128)(2,1)} %all-gather.18.cloned.1.call-done), kind=kOutput, calls=%fused_computation.60 | convolution fusion | flops 5951717376 | bytes 48234496 | tf_op jit(solution)/shard_map/dot_general | solution.py:72
  390.2 11.1 convolution_convert_fusion.1
  401.4 11.0 convolution_convert_fusion.2
  412.5 11.6 convolution_convert_fusion
  427.7 11.2 fusion.84
  438.9 21.1 %reduce-scatter.18.cloned.1.call-done = bf16[1024,352]{0,1:T(8,128)(2,1)} async-done(((bf16[1024,2816]{0,1:T(8,128)(2,1)}), bf16[1024,352]{0,1:T(8,128)(2,1)}) %reduce-scatter.18.cloned.1.call-update) | async-done | bytes 720912 | tf_op jit(solution)/shard_map/reduce_scatter | solution.py:241
  460.0 62.5 %reduce-scatter.16.cloned.1.call-done = bf16[1024,352]{0,1:T(8,128)(2,1)} async-done(((bf16[1024,2816]{0,1:T(8,128)(2,1)}), bf16[1024,352]{0,1:T(8,128)(2,1)}) %reduce-scatter.16.cloned.1.call-update) | async-done | bytes 720912 | tf_op jit(solution)/shard_map/reduce_scatter | solution.py:238
  522.5 62.5 %reduce-scatter.20.cloned.1.call-done = bf16[352,1024]{1,0:T(8,128)(2,1)} async-done(((bf16[2816,1024]{1,0:T(8,128)(2,1)}), bf16[352,1024]{1,0:T(8,128)(2,1)}) %reduce-scatter.20.cloned.1.call-update) | async-done | bytes 720912 | tf_op jit(solution)/shard_map/reduce_scatter | solution.py:244
  585.1 12.7 multiply_reduce_fusion.1
  604.9 7.2 fusion.63
  612.2 229.2 %while.29 = (s32[]{:T(128)}, f32[16,1024,64]{1,2,0:T(8,128)}, f32[16,1024,64]{1,2,0:T(8,128)}, f32[16,1024,64]{1,2,0:T(8,128)}, s32[16,1024]{1,0:T(8,128)}, /*in...) while((s32[]{:T(128)}, f32[16,1024,64]{1,2,0:T(8,128)}, ...), condition=%wide.region_11.12_spmd.clone, body=%wide.region_9.11_spmd.sunk.clone | while | flops 684850176 | bytes 34120812 | solution.py:212
  841.4 5.9 subtract_convert_fusion
  849.6 4.3 fusion.72
  856.8 4.4 fusion.74
  865.4 4.4 fusion.70
  869.8 4.2 copy.96
  874.0 6.7 fusion.86
  880.7 4.3 fusion.85
  885.0 9.6 fusion.53
  894.5 39.9 %all-reduce.4 = (f32[1024]{0:T(1024)S(1)}, f32[1024]{0:T(1024)S(1)}) all-reduce(f32[1024]{0:T(1024)S(1)} %get-tuple-element.227, f32[1024]{0:T(1024)S(1)} %get-tuple-element.225), channel_id=6, replica_groups=mesh['dp'=4,'hid'=2,'dm'=4] {'dp','hid','dm'}, use_global_device_ids=true, to_apply=%region_18.19.clone | all-reduce | flops 2048 | bytes 16384
  935.6 5.9 fusion.56
  941.5 3.9 copy.95
  945.5 10.6 add_convert_fusion
  964.7 54.9 %reduce-scatter.10.cloned.1.call-done = f32[32,1024]{1,0:T(8,128)} async-done(((f32[1024,1024]{1,0:T(8,128)}), f32[32,1024]{1,0:T(8,128)}) %reduce-scatter.10.cloned.1.call-update) | async-done | bytes 131088 | tf_op jit(solution)/shard_map/reduce_scatter | solution.py:255
  1019.5 141.2 %reduce-scatter.8.cloned.1.call-done = f32[32,1024]{1,0:T(8,128)} async-done(((f32[1024,1024]{1,0:T(8,128)}), f32[32,1024]{1,0:T(8,128)}) %reduce-scatter.8.cloned.1.call-update) | async-done | bytes 131088 | tf_op jit(solution)/shard_map/reduce_scatter | solution.py:254
  1160.7 141.2 %reduce-scatter.12.cloned.1.call-done = f32[32,1024]{1,0:T(8,128)} async-done(((f32[1024,1024]{1,0:T(8,128)}), f32[32,1024]{1,0:T(8,128)}) %reduce-scatter.12.cloned.1.call-update) | async-done | bytes 131088 | tf_op jit(solution)/shard_map/reduce_scatter | solution.py:256
  (409 shorter events, 426.5 us)
Async XLA Ops:
  7.2 139.8 %all-gather.8.cloned.1.call-start = ((), (), s32[]{:S(2)}) async-start(), calls=%async_computation.7 | async-start | bytes 2162688 | tf_op jit(solution)/shard_map/all_gather | solution.py:135
  7.9 33.0 %copy-start.28 = (bf16[32]{0:T(256)(128)(2,1)S(1)}, bf16[32]{0:T(256)(128)(2,1)}, u32[]{:S(2)}) copy-start(bf16[32]{0:T(256)(128)(2,1)} %param.21) | copy-start | bytes 196
  7.9 33.2 %copy-start.29 = (bf16[32]{0:T(256)(128)(2,1)S(1)}, bf16[32]{0:T(256)(128)(2,1)}, u32[]{:S(2)}) copy-start(bf16[32]{0:T(256)(128)(2,1)} %param.26) | copy-start | bytes 196
  7.9 153.3 %all-gather.10.cloned.1.call-start = ((), (), s32[]{:S(2)}) async-start(), calls=%async_computation.8 | async-start | bytes 2162688 | tf_op jit(solution)/shard_map/all_gather | solution.py:136
  8.7 327.5 %all-gather.12.cloned.1.call-start = ((), (), s32[]{:S(2)}) async-start(), calls=%async_computation.9 | async-start | bytes 2162688 | tf_op jit(solution)/shard_map/all_gather | solution.py:138
  9.4 334.0 %all-gather.14.cloned.1.call-start = ((), (), s32[]{:S(2)}) async-start(), calls=%async_computation.10 | async-start | bytes 6488064 | tf_op jit(solution)/shard_map/all_gather | solution.py:181
  10.0 346.4 %all-gather.16.cloned.1.call-start = ((), (), s32[]{:S(2)}) async-start(), calls=%async_computation.11 | async-start | bytes 6488064 | tf_op jit(solution)/shard_map/all_gather | solution.py:182
  10.6 357.8 %all-gather.18.cloned.1.call-start = ((), (), s32[]{:S(2)}) async-start(), calls=%async_computation.12 | async-start | bytes 6488064 | tf_op jit(solution)/shard_map/all_gather | solution.py:183
  10.6 8.7 collective-permute-start
  20.2 5.3 collective-permute-start.1
  26.3 7.9 collective-permute-start.2
  26.6 433.4 %reduce-scatter.18.cloned.1.call-start = ((), (), s32[]{:S(2)}) async-start(), calls=%async_computation.19 | async-start | bytes 6488064 | tf_op jit(solution)/shard_map/reduce_scatter | solution.py:241
  35.8 50.3 %collective-permute-start.3 = (bf16[256,1024]{1,0:T(8,128)(2,1)}, bf16[256,1024]{1,0:T(8,128)(2,1)S(1)}, u32[]{:S(2)}, u32[]{:S(2)}) collective-permute-start(bf16[256,1024]{1,0:T(8,128)(2,1)} %pad_maximum_fusion.2), channel_id=1, source_target_pairs={{0,24},{1,25},{2,26},{3,27},{4,28},{5,29},{6,30},{7,31},{8,0},{9,1... | collective-permute-start | bytes 1572872 | tf_op jit(solution)/shard_map/ppermute | solution.py:22
  37.9 47.9 %copy-start.30 = (s32[1,8]{1,0:T(1,128)S(1)}, s32[1,8]{1,0:T(1,128)}, u32[]{:S(2)}) copy-start(s32[1,8]{1,0:T(1,128)} %param.19) | copy-start | bytes 100
  37.9 48.1 %copy-start.8 = (bf16[32,1024]{1,0:T(8,128)(2,1)S(1)}, bf16[32,1024]{1,0:T(8,128)(2,1)}, u32[]{:S(2)}) copy-start(bf16[32,1024]{1,0:T(8,128)(2,1)} %param.24) | copy-start | bytes 196612
  40.9 295.4 %copy-start.1 = (bf16[1024,1024]{0,1:T(8,128)(2,1)}, bf16[1024,1024]{0,1:T(8,128)(2,1)S(1)}, u32[]{:S(2)}) copy-start(bf16[1024,1024]{0,1:T(8,128)(2,1)S(1)} %copy.79) | copy-start | bytes 6291460
  81.9 79.4 %copy-start.20 = (f32[1024]{0:T(1024)}, f32[1024]{0:T(1024)S(1)}, u32[]{:S(2)}) copy-start(f32[1024]{0:T(1024)S(1)} %convert_element_type.216) | copy-start | bytes 12292
  86.3 51.3 %collective-permute-start.4 = (bf16[512,1024]{1,0:T(8,128)(2,1)S(1)}, bf16[512,1024]{1,0:T(8,128)(2,1)S(1)}, u32[]{:S(2)}, u32[]{:S(2)}) collective-permute-start(bf16[512,1024]{1,0:T(8,128)(2,1)S(1)} %get-tuple-element.285), channel_id=1, source_target_pairs={{0,16},{1,17},{2,18},{3,19},{4,20},{5,21},{6,22},{7,23},{8,24},{9,... | collective-permute-start | bytes 3145736 | tf_op jit(solution)/shard_map/ppermute | solution.py:22
  91.1 46.8 %copy-start.10 = (bf16[1024,1024]{0,1:T(8,128)(2,1)S(1)}, bf16[1024,1024]{0,1:T(8,128)(2,1)}, u32[]{:S(2)}) copy-start(bf16[1024,1024]{0,1:T(8,128)(2,1)} %copy.80) | copy-start | bytes 6291460
  92.1 69.1 %copy-start.22 = (f32[1024]{0:T(1024)}, f32[1024]{0:T(1024)S(1)}, u32[]{:S(2)}) copy-start(f32[1024]{0:T(1024)S(1)} %fusion.67) | copy-start | bytes 12292
  93.3 72.3 %copy-start.15 = (f32[1024,32]{0,1:T(8,128)}, f32[1024,32]{0,1:T(8,128)S(1)}, u32[]{:S(2)}) copy-start(f32[1024,32]{0,1:T(8,128)S(1)} %get-tuple-element.301) | copy-start | bytes 393220
  161.3 4.4 copy-start.7
  181.2 1.9 copy-start
  190.9 1.9 copy-start
  239.8 1.9 copy-start
  249.7 1.9 copy-start
  318.2 1.9 copy-start
  336.2 4.9 copy-start.19
  356.3 12.0 copy-start.9
  401.3 121.2 %reduce-scatter.16.cloned.1.call-start = ((), (), s32[]{:S(2)}) async-start(), calls=%async_computation.18 | async-start | bytes 6488064 | tf_op jit(solution)/shard_map/reduce_scatter | solution.py:238
  412.4 172.6 %reduce-scatter.20.cloned.1.call-start = ((), (), s32[]{:S(2)}) async-start(), calls=%async_computation.20 | async-start | bytes 6488064 | tf_op jit(solution)/shard_map/reduce_scatter | solution.py:244
  424.1 460.8 %all-gather.20.cloned.1.call-start = ((), (), s32[]{:S(2)}) async-start(), calls=%async_computation.13 | async-start | bytes 2162688 | tf_op jit(solution)/shard_map/all_gather | solution.py:205
  424.7 533.8 %all-reduce.9.cloned.1.call-start = ((), (), s32[]{:S(2)}) async-start(), calls=%async_computation.21 | async-start | bytes 4325376 | tf_op jit(solution)/shard_map/psum | solution.py:249
  585.0 379.7 %reduce-scatter.14.cloned.1.call-start = ((), (), s32[]{:S(2)}) async-start(), calls=%async_computation.17 | async-start | bytes 4325376 | tf_op jit(solution)/shard_map/reduce_scatter | solution.py:257
  585.0 12.7 copy-start.6
  599.4 2.3 copy-start.4
  612.1 407.4 %reduce-scatter.10.cloned.1.call-start = ((), (), s32[]{:S(2)}) async-start(), calls=%async_computation.15 | async-start | bytes 4325376 | tf_op jit(solution)/shard_map/reduce_scatter | solution.py:255
  612.2 229.3 %copy-start.16 = (f32[1024,32]{0,1:T(8,128)S(1)}, f32[1024,32]{0,1:T(8,128)}, u32[]{:S(2)}) copy-start(f32[1024,32]{0,1:T(8,128)} %copy-done.15) | copy-start | bytes 393220
  612.2 229.2 %copy-start.18 = (f32[1024,32]{0,1:T(8,128)S(1)}, f32[1024,32]{0,1:T(8,128)}, u32[]{:S(2)}) copy-start(f32[1024,32]{0,1:T(8,128)} %get-tuple-element.299) | copy-start | bytes 393220
  847.3 2.3 copy-start.2
  847.3 2.3 copy-start.21
  847.3 2.3 copy-start.23
  854.0 306.8 %reduce-scatter.8.cloned.1.call-start = ((), (), s32[]{:S(2)}) async-start(), calls=%async_computation.14 | async-start | bytes 4325376 | tf_op jit(solution)/shard_map/reduce_scatter | solution.py:254
  861.2 440.7 %reduce-scatter.12.cloned.1.call-start = ((), (), s32[]{:S(2)}) async-start(), calls=%async_computation.16 | async-start | bytes 4325376 | tf_op jit(solution)/shard_map/reduce_scatter | solution.py:256
  874.0 6.7 copy-start.13
  874.0 6.7 copy-start.26
  885.0 50.6 %copy-start.25 = (f32[1024]{0:T(1024)S(1)}, f32[1024]{0:T(1024)}, u32[]{:S(2)}) copy-start(f32[1024]{0:T(1024)} %copy-done.24) | copy-start | bytes 12292
  958.6 4.8 copy-start.17
  (18 other events, 30.6 us)
Sparse Core Ops, SparseCore 0:
  10.8 66.5 all-gather.7
  80.3 80.9 all-gather.9
  164.1 55.0 all-gather.11
  221.0 42.0 all-gather.13
  264.8 43.1 all-gather.15
  309.8 43.1 all-gather.17
  401.4 58.5 reduce-scatter.17
  463.5 58.9 reduce-scatter.15
  525.9 58.9 reduce-scatter.19
  587.7 56.2 all-gather.19
  646.5 87.1 all-reduce.8
  736.5 141.5 reduce-scatter.13
  880.9 138.6 reduce-scatter.9
  1022.2 138.4 reduce-scatter.7
  1163.4 138.4 reduce-scatter.11
